TPU v7x, 8 devices: a whole 2x2x1 slice. The times are simulated.
8 devices in a mesh: dp: 2 (over y, z), ep: 4 (over x, core).
Axes of the slice: x: 2, y: 2, z: 1, core: 2. Of those that a mesh axis runs over, the one named last changes fastest.
Arguments:
- x: bfloat16 [2, 4, 256, 6144], P('dp', 'ep'), parts along dimension 0
- expert: int32 [2, 4, 256, 4], P('dp', 'ep'), parts along dimension 0
- slot: int32 [2, 4, 256, 4], P('dp', 'ep'), parts along dimension 0
- gate: float32 [2, 4, 256, 4], P('dp', 'ep'), parts along dimension 0
- w_gate: bfloat16 [8, 6144, 10752], P('ep')
- w_up: bfloat16 [8, 6144, 10752], P('ep')
- w_down: bfloat16 [8, 10752, 6144], P('ep')
Outputs:
- y: bfloat16 [2, 4, 256, 6144], P('dp', 'ep'), parts along dimension 0
There are 2 independent parts. A program takes and returns all parts, laid end to end along the dimension named above; an argument that names none is the same for every part.
All inputs are finite; a program needn't handle non-finite values.
Results may differ from a plain program's by a relative error of at most 0.009.
Values are sent between devices in bfloat16 or wider.
A program may use at most 2 GiB of HBM per device.

v0:
```python
import jax
import jax.numpy as jnp
from jax import lax
from jax.sharding import NamedSharding, PartitionSpec as P


def einsum(form, a, b):
    return jnp.einsum(form, a.astype(jnp.float32), b.astype(jnp.float32))


def solution(mesh):
    def placed(v, *spec):
        return lax.with_sharding_constraint(v, NamedSharding(mesh, P(*spec)))

    def step(x, expert, slot, gate, w_gate, w_up, w_down):
        experts, (tokens, top) = w_gate.shape[0], expert.shape[2:]
        slots = 5 * tokens * top // (4 * experts)
        to_expert = jax.nn.one_hot(expert, experts, dtype=jnp.bfloat16)
        to_slot = jax.nn.one_hot(slot, slots, dtype=jnp.bfloat16)
        weighted = to_expert * gate[..., None].astype(jnp.bfloat16)
        dispatch = einsum("abtke,abtkc->abtec", to_expert, to_slot).astype(jnp.bfloat16)
        combine = einsum("abtke,abtkc->abtec", weighted, to_slot).astype(jnp.bfloat16)
        z = einsum("abtec,abtd->aebcd", dispatch, x).astype(jnp.bfloat16)
        z = placed(z, "dp", None, "ep", None, None)
        z = placed(z, "dp", "ep", None, None, None)
        h = jax.nn.silu(einsum("aebcd,edf->aebcf", z, w_gate))
        h = (h * einsum("aebcd,edf->aebcf", z, w_up)).astype(jnp.bfloat16)
        out = einsum("aebcf,efd->aebcd", h, w_down).astype(jnp.bfloat16)
        out = placed(out, "dp", "ep", None, None, None)
        out = placed(out, "dp", None, "ep", None, None)
        y = einsum("abtec,aebcd->abtd", combine, out)
        return y.astype(jnp.bfloat16)

    return step
```

profile of v0, /device:TPU:0, one launch (start us, length us, event | category | flops | bytes accessed | tf_op | source)
XLA Modules:
  0.0 956.6 jit_solution(12293022643424524947)
XLA Ops:
  0.0 0.0 copy-start
  0.0 1.0 copy.11
  1.0 0.0 copy-start.2
  1.0 0.8 copy.9
  1.8 0.0 copy-start.4
  1.8 2.6 convolution_convert_fusion.1
  4.4 0.0 copy-done
  4.4 9.1 convolution_convert_fusion
  13.5 183.4 %all-to-all.4 = bf16[1,4,2,1,160,6144]{5,4,2,3,0,1:T(8,128)(2,1)} all-to-all(bf16[1,4,2,1,160,6144]{5,4,2,3,0,1:T(8,128)(2,1)} %bitcast.121), channel_id=1, replica_groups=mesh['dp'=2,'ep'=4] {'ep'}, dimensions={1} | all-to-all | bytes 31457280 | tf_op jit(solution)/sharding_constraint;jit(solution)/sharding_constraint | solution.py:13
  197.0 0.0 copy-done.2
  197.0 0.0 copy-done.4
  197.0 183.2 %fusion.2 = f32[2,4,160,10752]{3,2,1,0:T(8,128)} fusion(bf16[2,6144,10752]{2,1,0:T(8,128)(2,1)} %param.5, bf16[1,4,2,1,160,6144]{5,4,2,3,0,1:T(8,128)(2,1)} %all-to-all.4), kind=kOutput, calls=%fused_computation.2 | convolution fusion | flops 169114337280 | bytes 335020032 | tf_op jit(solution)/aebcd,edf->aebcf/dot_general | solution.py:8
  380.2 188.9 %fusion.61 = bf16[2,4,160,10752]{3,2,1,0:T(8,128)(2,1)} fusion(f32[2,4,160,10752]{3,2,1,0:T(8,128)} %fusion.2, bf16[2,6144,10752]{2,1,0:T(8,128)(2,1)} %param.4, bf16[1,4,2,1,160,6144]{5,4,2,3,0,1:T(8,128)(2,1)} %all-to-all.4), kind=kOutput, calls=%fused_computation.13.clone.clone.clone.1 | convolution fusion | flops 169196912640 | bytes 362545152 | tf_op jit(solution)/aebcd,edf->aebcf/dot_general | solution.py:8
  569.0 184.0 %convert_bitcast_fusion = bf16[1,2,4,1,160,6144]{5,4,2,1,3,0:T(8,128)(2,1)} fusion(bf16[2,10752,6144]{2,1,0:T(8,128)(2,1)} %param.6, bf16[2,4,160,10752]{3,2,1,0:T(8,128)(2,1)} %fusion.61), kind=kOutput, calls=%fused_computation.16 | convolution fusion | flops 169122201600 | bytes 307494912 | tf_op jit(solution)/aebcf,efd->aebcd/dot_general | solution.py:8
  753.0 13.4 %copy.15 = bf16[1,2,4,1,160,6144]{5,4,1,3,0,2:T(8,128)(2,1)} copy(bf16[1,2,4,1,160,6144]{5,4,2,1,3,0:T(8,128)(2,1)} %convert_bitcast_fusion) | data formatting | bytes 31457280 | tf_op jit(solution)/sharding_constraint;jit(solution)/sharding_constraint | solution.py:13
  766.4 6.8 all-to-all-start.1
  773.3 0.0 copy-done.6
  773.3 0.0 copy-start.1
  773.3 0.1 copy.10
  773.5 0.0 copy-done.3
  773.5 0.0 copy-done.5
  773.5 3.1 convolution_convert_fusion.2
  776.6 168.2 %all-to-all-done.1 = bf16[1,2,4,1,160,6144]{5,4,1,3,0,2:T(8,128)(2,1)} async-done(((bf16[1,2,4,1,160,6144]{5,4,1,3,0,2:T(8,128)(2,1)}), bf16[1,2,4,1,160,6144]{5,4,1,3,0,2:T(8,128)(2,1)}, u32[]{:S(2)}, u32[]{:S(2)}) %all-to-all-start.1) | async-done | bytes 15728672 | tf_op jit(solution)/sharding_constraint;jit(solution)/sharding_constraint | solution.py:13
  944.8 11.8 %fusion.31 = bf16[1,1,256,6144]{3,2,1,0:T(8,128)(2,1)} fusion(bf16[8,160,6144]{2,1,0:T(8,128)(2,1)} %bitcast.25, bf16[256,8,160]{2,1,0:T(8,128)(2,1)} %convolution_convert_fusion.2), kind=kOutput, calls=%fused_computation.22 | convolution fusion | flops 4028104704 | bytes 19529728 | tf_op jit(solution)/abtec,aebcd->abtd/dot_general | solution.py:8
  (5 shorter events, 0.0 us)
Async XLA Ops:
  0.0 4.4 copy-start
  1.0 196.0 %copy-start.2 = (s32[256,4]{1,0:T(8,128)}, s32[256,4]{1,0:T(8,128)S(1)}, u32[]{:S(2)}) copy-start(s32[256,4]{1,0:T(8,128)S(1)} %copy.11) | copy-start | bytes 12292
  1.8 195.1 %copy-start.4 = (s32[256,4]{1,0:T(8,128)}, s32[256,4]{1,0:T(8,128)S(1)}, u32[]{:S(2)}) copy-start(s32[256,4]{1,0:T(8,128)S(1)} %copy.9) | copy-start | bytes 12292
  753.0 20.3 %copy-start.6 = (f32[1,1,256,4]{2,3,1,0:T(4,128)S(1)}, f32[1,1,256,4]{2,3,1,0:T(4,128)}, u32[]{:S(2)}) copy-start(f32[1,1,256,4]{2,3,1,0:T(4,128)} %param.1) | copy-start | bytes 12292
  753.0 20.4 %copy-start.3 = (s32[256,4]{1,0:T(8,128)S(1)}, s32[256,4]{1,0:T(8,128)}, u32[]{:S(2)}) copy-start(s32[256,4]{1,0:T(8,128)} %copy-done.2) | copy-start | bytes 12292
  753.0 20.4 %copy-start.5 = (s32[256,4]{1,0:T(8,128)S(1)}, s32[256,4]{1,0:T(8,128)}, u32[]{:S(2)}) copy-start(s32[256,4]{1,0:T(8,128)} %copy-done.4) | copy-start | bytes 12292
  766.4 178.3 %all-to-all-start.1 = ((bf16[1,2,4,1,160,6144]{5,4,1,3,0,2:T(8,128)(2,1)}), bf16[1,2,4,1,160,6144]{5,4,1,3,0,2:T(8,128)(2,1)}, u32[]{:S(2)}, u32[]{:S(2)}) async-start(bf16[1,2,4,1,160,6144]{5,4,1,3,0,2:T(8,128)(2,1)} %copy.15), calls=%async_computation.1 | async-start | bytes 31457280 | tf_op jit(solution)/sharding_constraint;jit(solution)/sharding_constraint | solution.py:13
  773.3 183.3 %copy-start.1 = (bf16[1,1,256,6144]{3,2,1,0:T(8,128)(2,1)S(1)}, bf16[1,1,256,6144]{3,2,1,0:T(8,128)(2,1)}, u32[]{:S(2)}) copy-start(bf16[1,1,256,6144]{3,2,1,0:T(8,128)(2,1)} %param.3) | copy-start | bytes 9437188
where the time goes:
time: 957 us
  matrix products  583 us (61%)
  blocking collectives  183 us (19%)
  waiting for transfers between devices  168 us (18%)
  local copies, waits for them, and re-layouts  15.4 us (2%)
    dot_general x7, matrix products, einsum(): return jnp.einsum(form, a.astype(jnp.float32), b.astype(jnp.float32))  583 us
    another operation x1, blocking collectives, placed(): return lax.with_sharding_constraint(v, NamedSharding(mesh, P(*spec)))  183 us
    another operation x1, waiting for transfers between devices, placed(): return lax.with_sharding_constraint(v, NamedSharding(mesh, P(*spec)))  168 us
  transfers between devices with their start and end apart: 1, of which 1 were waited for; matrix products, arithmetic and copies ran while one was open for 0% of the time, Pallas kernels for 0%

commit v1 on v0

v1 whole, which is shorter than its diff:
```python
import functools

import jax
import jax.numpy as jnp
from jax import lax
from jax.experimental import pallas as pl
from jax.experimental.pallas import tpu as pltpu
from jax.sharding import PartitionSpec as P


F32, BF16, I32 = jnp.float32, jnp.bfloat16, jnp.int32
MESH = pl.DeviceIdType.MESH
VMEM_LIMIT = 62 * 2**20
CHUNKS = (1536, 1536, 1536, 1024, 512)
NEAR_BLOCK, REST_BLOCK, DOWN_BLOCK = 512, 512, 256
NEAR_SIZES = (192, 256, 320)
NEAR_STEPS = 15
ROW_CHUNKS = (192, 224, 256, 288, 320)
SOURCES = 6
FIRST, SECOND, NEAR, ROWS, START, COUNT = 0, 1, 2, 3, 8, 24


def cost(flops, nbytes):
    return pl.CostEstimate(flops=int(flops), bytes_accessed=int(nbytes), transcendentals=0)


def plan_kernel(slots, expert_ref, slot_ref, gate_ref, pos_ref, scale_ref, num_ref, mine, got, send, recv):
    dp, ep = lax.axis_index("dp"), lax.axis_index("ep")
    tokens = expert_ref.shape[1]

    def peer(i):
        return (dp ^ (i // 4), ep ^ (i % 4))

    expert, slot = expert_ref[...], slot_ref[...]
    gate = gate_ref[...].astype(BF16).astype(F32)
    for pair in range(4):
        rows = []
        for e in (2 * pair, 2 * pair + 1):
            hit = (expert == e) & (slot < slots)
            rows.append(jnp.sum(jnp.where(hit, 1.0, 0.0), 0, keepdims=True))
            rows.append(jnp.sum(jnp.where(hit, gate, 0.0), 0, keepdims=True))
        rows = [rows[0], rows[2], rows[1], rows[3], jnp.zeros((4, tokens), F32)]
        mine[pair] = jnp.concatenate(rows, 0)

    barrier = pltpu.get_barrier_semaphore()
    for i in range(1, 8):
        pl.semaphore_signal(barrier, inc=1, device_id=peer(i), device_id_type=MESH)
    pl.semaphore_wait(barrier, 7)
    copies = []
    for i in range(1, 8):
        copies.append(
            pltpu.make_async_remote_copy(
                src_ref=mine.at[ep ^ (i % 4)],
                dst_ref=got.at[i],
                send_sem=send.at[i],
                recv_sem=recv.at[i],
                device_id=peer(i),
                device_id_type=MESH,
            )
        )
    for copy in copies:
        copy.start()
    for copy in copies:
        copy.wait()

    blocks = [mine[ep]] + [got[i] for i in range(1, 8)]
    valid = jnp.concatenate([b[0:2] for b in blocks], 0)
    scales = [b[2:4] for b in blocks]
    upper = lax.broadcasted_iota(I32, (tokens, tokens), 0) <= lax.broadcasted_iota(I32, (tokens, tokens), 1)
    upto = jnp.dot(valid.astype(BF16), upper.astype(F32).astype(BF16), preferred_element_type=F32)

    results = []
    for e in range(2):
        v = [valid[2 * i + e : 2 * i + e + 1] > 0.0 for i in range(8)]
        rank = [upto[2 * i + e : 2 * i + e + 1] - 1.0 for i in range(8)]
        c = [r[:, tokens - 1 :] + 1.0 for r in rank]
        near, other = c[0] + c[1], c[4] + c[5]
        gap = near + c[2] + c[3] - other - c[6] - c[7]
        give = jnp.minimum(jnp.maximum(jnp.floor(gap * 0.5), 0.0), near)
        take = jnp.minimum(jnp.maximum(jnp.floor(-gap * 0.5), 0.0), other)
        keep, skip = near - give, other - take
        counts = [jnp.minimum(c[0], keep)]
        counts += [keep - counts[0], c[2], c[3], jnp.maximum(c[4] - skip, 0.0)]
        counts += [take - counts[4]]
        starts = [jnp.zeros_like(keep)]
        for n in counts:
            starts.append(starts[-1] + n)
        place = [rank[0], rank[1] + c[0], rank[2] + starts[2], rank[3] + starts[3]]
        mine_too = [v[0] & (place[0] < keep), v[1] & (place[1] < keep), v[2], v[3]]
        for i, n in ((4, rank[4]), (5, rank[5] + c[4])):
            mine_too.append(v[i] & (n >= skip))
            place.append(n - skip + starts[4])
        pos = [jnp.where(m, p, -1.0) for m, p in zip(mine_too, place)]
        results.append((keep, starts[6], starts[:6], counts, pos, [s[e : e + 1] for s in scales[:6]]))

    swap = results[1][0] > results[0][0]

    def pick(a, b):
        return jnp.where(swap, b, a), jnp.where(swap, a, b)

    (a_keep, a_rows, a_starts, a_counts, a_pos, a_scale), (b_keep, b_rows, b_starts, b_counts, b_pos, b_scale) = results
    pad = jnp.full((2, tokens), -1.0, F32)
    pos = [pick(a, b) for a, b in zip(a_pos, b_pos)]
    scale = [pick(a, b) for a, b in zip(a_scale, b_scale)]
    pos_ref[...] = jnp.concatenate([p[0] for p in pos] + [pad] + [p[1] for p in pos] + [pad], 0).astype(I32)
    scale_ref[...] = jnp.concatenate([p[0] for p in scale] + [pad] + [p[1] for p in scale] + [pad], 0)
    lane = lax.broadcasted_iota(I32, (1, 128), 1)
    numbers = {FIRST: jnp.where(swap, 1.0, 0.0), SECOND: jnp.where(swap, 0.0, 1.0)}
    numbers[NEAR] = pick(a_keep, b_keep)[0]
    numbers[ROWS], numbers[ROWS + 1] = pick(a_rows, b_rows)
    for s in range(SOURCES):
        numbers[START + s], numbers[START + 8 + s] = pick(a_starts[s], b_starts[s])
        numbers[COUNT + s], numbers[COUNT + 8 + s] = pick(a_counts[s], b_counts[s])
    out = jnp.zeros((1, 128), F32)
    for at, value in numbers.items():
        out = jnp.where(lane == at, value, out)
    num_ref[...] = out.astype(I32)


def plan(expert, slot, gate, slots):
    tokens = expert.shape[1]
    return pl.pallas_call(
        functools.partial(plan_kernel, slots),
        out_shape=[
            jax.ShapeDtypeStruct((16, tokens), I32),
            jax.ShapeDtypeStruct((16, tokens), F32),
            jax.ShapeDtypeStruct((1, 128), I32),
        ],
        scratch_shapes=[
            pltpu.VMEM((4, 8, tokens), F32),
            pltpu.VMEM((8, 8, tokens), F32),
            pltpu.SemaphoreType.DMA((8,)),
            pltpu.SemaphoreType.DMA((8,)),
        ],
        cost_estimate=cost(10**7, 10**5),
        compiler_params=pltpu.CompilerParams(collective_id=0, has_side_effects=True),
        name="plan",
    )(expert, slot, gate)


def floor16(n):
    return n // 16 * 16


def place_rows(window, x_ref, pos, start, count, z_ref, block=2048):
    tokens, d = x_ref.shape
    low = pl.multiple_of(floor16(start), 16)

    @pl.when(count > 0)
    def _():
        rows = lax.broadcasted_iota(I32, (window, tokens), 0) + low
        pick = (rows == pos).astype(F32).astype(BF16)

        def step(k, _):
            at = pl.ds(pl.multiple_of(k * block, block), block)
            z = jnp.dot(pick, x_ref[:, at], preferred_element_type=F32).astype(BF16)
            z_ref[pl.ds(low, 16), at] += z[:16]
            z_ref[pl.ds(pl.multiple_of(low + 16, 16), window - 16), at] = z[16:]
            return 0

        lax.fori_loop(0, d // block, step, 0)


def sizes_do(sizes, n, body):
    for k, size in enumerate(sizes):
        low = n > sizes[k - 1] if k else n >= 0
        high = n <= size if k + 1 < len(sizes) else n >= 0
        pl.when(low & high)(functools.partial(body, size))


def chunks_do(rows, body):
    single = [c for c in ROW_CHUNKS if c % 64 == 0]
    for c in ROW_CHUNKS:
        two = (rows > max(2 * c - 64, ROW_CHUNKS[-1])) & (rows <= 2 * c)
        use = two
        if c in single:
            k = single.index(c)
            use = two | ((rows > (single[k - 1] if k else -1)) & (rows <= c))
        pl.when(use)(functools.partial(body, c, jnp.where(two, 2, 1)))


def swiglu(z, wg, wu):
    g = jnp.dot(z, wg, preferred_element_type=F32)
    u = jnp.dot(z, wu, preferred_element_type=F32)
    return (jax.nn.silu(g) * u).astype(BF16)


def up_near_kernel(window, num, x_ref, mate_ref, pos_ref, scale_ref, wg_ref, wu_ref, h_ref, mix_ref, z):
    j = pl.program_id(0)
    tokens = x_ref.shape[0]

    @pl.when((j > 0) & (j <= 2 * SOURCES))
    def _():
        k = j - 1
        row = k // SOURCES * 8 + lax.rem(k, SOURCES)
        at = lax.broadcasted_iota(I32, (window, tokens), 0) + floor16(num[START + row])
        weight = jnp.where(at == pos_ref[pl.ds(row, 1), :], scale_ref[pl.ds(row, 1), :], 0.0)
        mix_ref[k] = weight.T.astype(BF16)

    @pl.when(j == 0)
    def _():
        z[...] = jnp.zeros_like(z)
        for s, ref in enumerate((x_ref, mate_ref)):
            place_rows(window, ref, pos_ref[s : s + 1, :], num[START + s], num[COUNT + s], z)

    def body(m):
        h_ref[0:m] = swiglu(z[0:m], wg_ref[...], wu_ref[...])
        if m < h_ref.shape[0]:
            h_ref[m:] = jnp.zeros((h_ref.shape[0] - m, h_ref.shape[1]), BF16)

    sizes_do(NEAR_SIZES, num[NEAR], body)


def up_near(num, x, mate, pos, scale, wg, wu, slots):
    tokens, d = x.shape
    window, rows = slots + 16, NEAR_SIZES[-1]
    whole = pl.BlockSpec((tokens, d), lambda j, num: (0, 0), pipeline_mode=pl.Buffered(1))
    weights = pl.BlockSpec((None, d, NEAR_BLOCK), lambda j, num: (num[FIRST], 0, j))
    return pl.pallas_call(
        functools.partial(up_near_kernel, window),
        out_shape=[
            jax.ShapeDtypeStruct((rows, NEAR_STEPS * NEAR_BLOCK), BF16),
            jax.ShapeDtypeStruct((2 * SOURCES, tokens, window), BF16),
        ],
        grid_spec=pltpu.PrefetchScalarGridSpec(
            num_scalar_prefetch=1,
            grid=(NEAR_STEPS,),
            in_specs=[whole, whole]
            + [pl.BlockSpec(pos.shape, lambda j, num: (0, 0))] * 2
            + [weights, weights],
            out_specs=[
                pl.BlockSpec((rows, NEAR_BLOCK), lambda j, num: (0, j)),
                pl.BlockSpec((2 * SOURCES, tokens, window), lambda j, num: (0, 0, 0)),
            ],
            scratch_shapes=[pltpu.VMEM((rows + window, d), BF16)],
        ),
        cost_estimate=cost(4 * rows * d * NEAR_STEPS * NEAR_BLOCK, 4 * d * NEAR_STEPS * NEAR_BLOCK),
        compiler_params=pltpu.CompilerParams(vmem_limit_bytes=VMEM_LIMIT),
        name="up_near",
    )(num, x, mate, pos, scale, wg, wu)


def up_rest_kernel(window, steps, num, *refs):
    sources, (pos_ref, near_ref, wg_ref, wu_ref, one_ref, two_ref), xs = (
        refs[:SOURCES],
        refs[SOURCES : SOURCES + 6],
        refs[SOURCES + 6 : 2 * SOURCES + 6],
    )
    z, sems = refs[2 * SOURCES + 6 :]
    j = pl.program_id(0)
    copies = [pltpu.make_async_copy(sources[s], xs[s], sems.at[s]) for s in range(SOURCES)]

    def fill(e, fresh):
        z[...] = jnp.zeros_like(z)
        for s in range(SOURCES):
            if fresh:
                copies[s].wait()
            row = 8 * e + s
            place_rows(window, xs[s], pos_ref[row : row + 1, :], num[START + row], num[COUNT + row], z)

    @pl.when(j == 0)
    def _():
        for copy in copies:
            copy.start()
        fill(0, True)

    @pl.when(j == steps)
    def _():
        fill(1, False)

    near_rows = near_ref.shape[0]
    first = j < steps
    base = jnp.where(j < NEAR_STEPS, floor16(num[NEAR]), 0)
    rows = jnp.where(first, num[ROWS] - base, num[ROWS + 1])

    @pl.when(first)
    def _():
        one_ref[0:near_rows] = near_ref[...]
        one_ref[near_rows:] = jnp.zeros((one_ref.shape[0] - near_rows, one_ref.shape[1]), BF16)

    @pl.when(jnp.logical_not(first))
    def _():
        two_ref[...] = jnp.zeros_like(two_ref)

    def body(c, n):
        def chunk(t, _):
            at = pl.ds(pl.multiple_of(base + t * c, 16), c)
            h = swiglu(z[at], wg_ref[...], wu_ref[...])

            @pl.when(first)
            def _():
                one_ref[at] = h

            @pl.when(jnp.logical_not(first))
            def _():
                two_ref[at] = h

            return 0

        lax.fori_loop(0, n, chunk, 0)

    chunks_do(rows, body)


def up_rest(num, sources, pos, near, wg, wu, slots):
    tokens, d = sources[0].shape
    ff = wg.shape[2]
    window, rows = slots + 16, 2 * ROW_CHUNKS[-1]
    steps = ff // REST_BLOCK
    weights = pl.BlockSpec(
        (None, d, REST_BLOCK),
        lambda j, num: (jnp.where(j < steps, num[FIRST], num[SECOND]), 0, lax.rem(j, steps)),
    )
    early = lambda j, num: (0, jnp.minimum(j, steps - 1))
    late = lambda j, num: (0, jnp.maximum(j - steps, 0))
    return pl.pallas_call(
        functools.partial(up_rest_kernel, window, steps),
        out_shape=[jax.ShapeDtypeStruct((rows + 128, ff), BF16), jax.ShapeDtypeStruct((rows, ff), BF16)],
        grid_spec=pltpu.PrefetchScalarGridSpec(
            num_scalar_prefetch=1,
            grid=(2 * steps,),
            in_specs=[pl.BlockSpec(memory_space=pl.ANY)] * SOURCES
            + [
                pl.BlockSpec(pos.shape, lambda j, num: (0, 0)),
                pl.BlockSpec((near.shape[0], REST_BLOCK), lambda j, num: (0, jnp.minimum(j, NEAR_STEPS - 1))),
                weights,
                weights,
            ],
            out_specs=[pl.BlockSpec((rows + 128, REST_BLOCK), early), pl.BlockSpec((rows, REST_BLOCK), late)],
            scratch_shapes=[pltpu.VMEM((tokens, d), BF16)] * SOURCES
            + [pltpu.VMEM((rows + window, d), BF16), pltpu.SemaphoreType.DMA((SOURCES,))],
        ),
        cost_estimate=cost(6 * rows * d * ff, 8 * d * ff),
        compiler_params=pltpu.CompilerParams(vmem_limit_bytes=VMEM_LIMIT),
        name="up_rest",
    )(num, *sources, pos, near, wg, wu)


def down_kernel(num, begin, one_ref, two_ref, mix, w_ref, *refs):
    outs, (h, out, acc, sems) = refs[:SOURCES], refs[SOURCES:]
    e, j = pl.program_id(0), pl.program_id(1)
    window = mix.shape[2]
    columns = pl.ds(pl.multiple_of(j * DOWN_BLOCK, DOWN_BLOCK), DOWN_BLOCK)
    start = (e == 0) & (j == 0)

    def load(k, c, t):
        at = pl.ds(pl.multiple_of(t * c, 32), c)
        return pltpu.make_async_copy((one_ref, two_ref)[k].at[at], h.at[k, at], sems.at[k, t])

    @pl.when(start)
    def _():
        out[...] = jnp.zeros_like(out)

    @pl.when((e == 0) & (j == 1))
    def _():
        def body(c, n):
            load(1, c, 0).start()
            pl.when(n > 1)(lambda: load(1, c, 1).start())

        chunks_do(num[ROWS + 1], body)

    def body(c, n):
        pl.when(start)(lambda: load(0, c, 0).start())

        def chunk(t, _):
            @pl.when(start)
            def _():
                load(0, c, t).wait()
                pl.when(t + 1 < n)(lambda: load(0, c, t + 1).start())

            pl.when((e == 1) & (j == 0))(lambda: load(1, c, t).wait())
            at = pl.ds(pl.multiple_of(t * c, 32), c)
            out[at] = jnp.dot(h[e, at], w_ref[...], preferred_element_type=F32).astype(BF16)
            return 0

        lax.fori_loop(0, n, chunk, 0)

    chunks_do(num[ROWS + e], body)

    def term(s):
        low = pl.multiple_of(floor16(num[START + 8 * e + s]), 16)
        return jnp.dot(mix[e * SOURCES + s], out[pl.ds(low, window)], preferred_element_type=F32)

    @pl.when(e == 0)
    def _():
        for s in range(SOURCES):
            acc[s, :, columns] = term(s)

    @pl.when(e == 1)
    def _():
        for s in range(SOURCES):
            outs[s][...] = (acc[s, :, columns] + term(s)).astype(outs[s].dtype)


def down(num, begin, one, two, mix, w, size):
    tokens, window = mix.shape[1:]
    rows, ff = two.shape
    weights = pl.BlockSpec(
        (None, ff, DOWN_BLOCK), lambda e, j, num, begin: (num[FIRST + e], 0, begin[0] + j)
    )
    return pl.pallas_call(
        down_kernel,
        out_shape=[jax.ShapeDtypeStruct((tokens, size), F32 if s == 0 else BF16) for s in range(SOURCES)],
        grid_spec=pltpu.PrefetchScalarGridSpec(
            num_scalar_prefetch=2,
            grid=(2, size // DOWN_BLOCK),
            in_specs=[pl.BlockSpec(memory_space=pl.ANY)] * 2
            + [pl.BlockSpec(mix.shape, lambda e, j, num, begin: (0, 0, 0), pipeline_mode=pl.Buffered(1)), weights],
            out_specs=[pl.BlockSpec((tokens, DOWN_BLOCK), lambda e, j, num, begin: (0, e * j))] * SOURCES,
            scratch_shapes=[
                pltpu.VMEM((2, rows, ff), BF16),
                pltpu.VMEM((rows + window, DOWN_BLOCK), BF16),
                pltpu.VMEM((SOURCES, tokens, size), F32),
                pltpu.SemaphoreType.DMA((2, 2)),
            ],
        ),
        cost_estimate=cost(4 * rows * ff * size, 4 * ff * size + 4 * rows * ff),
        compiler_params=pltpu.CompilerParams(vmem_limit_bytes=VMEM_LIMIT),
        name="down",
    )(num, begin, one, two, mix, w)


def solution(mesh):
    members = mesh.shape["ep"]

    def swap(v, code):
        pairs = [(i, i ^ code) for i in range(2 * members)]
        return lax.ppermute(v, ("dp", "ep"), pairs)

    def layer(x, expert, slot, gate, w_gate, w_up, w_down):
        x, expert, slot, gate = x[0, 0], expert[0, 0], slot[0, 0], gate[0, 0]
        tokens, top = expert.shape
        slots = 5 * tokens * top // (4 * members * w_gate.shape[0])
        pos, scale, num = plan(expert.T, slot.T, gate.T, slots)
        num = num.reshape(128)
        mate = swap(x, 1)
        x, num = lax.optimization_barrier((x, num))
        far, across = swap(x, 2), swap(x, 4)
        near, mix = up_near(num, x, mate, pos, scale, w_gate, w_up, slots)
        far, across, near = lax.optimization_barrier((far, across, near))
        sources = (x, mate, far, swap(far, 1), across, swap(across, 1))
        one, two = up_rest(num, sources, pos, near, w_gate, w_up, slots)
        parts, start = [], 0
        for size in CHUNKS:
            y, *send = down(num, jnp.full((1,), start // DOWN_BLOCK, I32), one, two, mix, w_down, size)
            got = [swap(term, s + 1) for s, term in enumerate(send)]
            for term in got:
                y = y + term.astype(F32)
            parts.append(y.astype(BF16))
            start += size
        return jnp.concatenate(parts, 1)[None, None]

    tokens_spec = P("dp", "ep", None, None)
    weight_spec = P("ep", None, None)
    return jax.shard_map(
        layer,
        mesh=mesh,
        in_specs=(tokens_spec,) * 4 + (weight_spec,) * 3,
        out_specs=tokens_spec,
        check_vma=False,
    )
```

time: 957 us -> 690 us (0.72)
  matrix products: 583 us -> 0 us
  Pallas kernels: 0 us -> 474 us
  blocking collectives: 183 us -> 0 us
  starting transfers between devices: 6.84 us -> 128 us
  waiting for transfers between devices: 168 us -> 72.1 us
  local copies, waits for them, and re-layouts: 15.4 us -> 1.72 us
    dot_general x7 -> x0, matrix products: 583 us -> none  [einsum(): return jnp.einsum(form, a.astype(jnp.float32), b.astype(jnp.float32))]
    pallas_call x0 -> x8, Pallas kernels: none -> 474 us  [the longest x1 228 us: up_rest(): pl.pallas_call(functools.partial(up_rest_kernel, window, steps), out_shap...]
    another operation x1 -> x0, blocking collectives: 183 us -> none  [placed(): return lax.with_sharding_constraint(v, NamedSharding(mesh, P(*spec)))]
    another operation x1 -> x0, waiting for transfers between devices: 168 us -> none  [placed(): return lax.with_sharding_constraint(v, NamedSharding(mesh, P(*spec)))]
    ppermute x0 -> x30, starting transfers between devices: none -> 128 us  [swap(): return lax.ppermute(v, ('dp', 'ep'), pairs)]
    ppermute x0 -> x30, waiting for transfers between devices: none -> 72.1 us  [swap(): return lax.ppermute(v, ('dp', 'ep'), pairs)]
    another operation x1 -> x0, local copies, waits for them, and re-layouts: 13.4 us -> none  [placed(): return lax.with_sharding_constraint(v, NamedSharding(mesh, P(*spec)))]
  transfers between devices with their start and end apart: 1 -> 30, of which waited for: 1 -> 14; matrix products, arithmetic and copies ran while one was open for 0% -> 1% of each run, Pallas kernels for 0% -> 30%
where the time goes in v1:
time: 690 us; the launch traced here: 683 us
  Pallas kernels  474 us (69%)
  starting transfers between devices  128 us (19%)
  waiting for transfers between devices  72.1 us (10%)
  other arithmetic  7.08 us (1%)
    pallas_call x1, Pallas kernels, up_rest(): pl.pallas_call(functools.partial(up_rest_kernel, window, steps), out_shap...  228 us
    pallas_call x5, Pallas kernels, down(): pl.pallas_call(down_kernel, out_shape=[jax.ShapeDtypeStruct((tokens, size...  172 us
    ppermute x30, starting transfers between devices, swap(): return lax.ppermute(v, ('dp', 'ep'), pairs)  128 us
    ppermute x30, waiting for transfers between devices, swap(): return lax.ppermute(v, ('dp', 'ep'), pairs)  72.1 us
    pallas_call x1, Pallas kernels, up_near(): pl.pallas_call(functools.partial(up_near_kernel, window), out_shape=[jax....  66.5 us
  transfers between devices with their start and end apart: 30, of which 14 were waited for; matrix products, arithmetic and copies ran while one was open for 1% of the time, Pallas kernels for 30%

profile of v1, /device:TPU:0, one launch (start us, length us, event | category | flops | bytes accessed | tf_op | source)
XLA Modules:
  0.0 683.3 jit_solution(13167121913299472316)
XLA Ops:
  0.8 7.7 %plan.1 = (s32[16,256]{1,0:T(8,128)}, f32[16,256]{1,0:T(8,128)}, s32[1,128]{1,0:T(1,128)}) custom-call(s32[4,256]{1,0:T(4,128)} %bitcast.24, s32[4,256]{1,0:T(4,128)} %bitcast.25, f32[4,256]{1,0:T(4,128)} %bitcast.26), custom_call_target="tpu_custom_call" | custom-call | flops 10000000 | bytes 100000 | tf_op jit(solution)/shard_map/plan/pallas_call | solution.py:122
  11.9 66.5 %up_near.1 = (bf16[320,7680]{1,0:T(8,128)(2,1)}, bf16[12,256,176]{2,1,0:T(8,128)(2,1)}) custom-call(s32[128]{0:T(128)} %bitcast.17, bf16[256,6144]{1,0:T(8,128)(2,1)} %bitcast.15, bf16[256,6144]{1,0:T(8,128)(2,1)} %collective-permute-done.mate_ref.refs_1_, s32[16,256]{1,0:T(8,128)} %get-tuple-element.50.pos_ref.refs_6_, ...), custom_call_target="tpu_custom_call" | custom-call | flops 60397977600 | bytes 188743680 | tf_op jit(solution)/shard_map/up_near/pallas_call | solution.py:219
  80.5 10.0 %collective-permute-start.3 = (bf16[256,6144]{1,0:T(8,128)(2,1)}, bf16[256,6144]{1,0:T(8,128)(2,1)}, u32[]{:S(2)}, u32[]{:S(2)}) collective-permute-start(bf16[256,6144]{1,0:T(8,128)(2,1)} %collective-permute-done.1.refs_2_), channel_id=1, source_target_pairs={{0,1},{1,0},{2,3},{3,2},{4,5},{5,4},{6,7},{7,6}} | collective-permute-start | bytes 9437192 | tf_op jit(solution)/shard_map/ppermute | solution.py:428
  90.5 5.6 collective-permute-done.3.refs_3_
  96.1 4.5 collective-permute-done.4.refs_5_
  100.6 228.2 %up_rest.1 = (bf16[768,10752]{1,0:T(8,128)(2,1)}, bf16[640,10752]{1,0:T(8,128)(2,1)}) custom-call(s32[128]{0:T(128)} %bitcast.18, bf16[256,6144]{1,0:T(8,128)(2,1)} %bitcast.16, bf16[256,6144]{1,0:T(8,128)(2,1)} %collective-permute-done.mate_ref.refs_1_, bf16[256,6144]{1,0:T(8,128)(2,1)} %collective-permute-done.1.refs_2_, ...), custom_call_target="tpu_custom_call" | custom-call | flops 253671505920 | bytes 528482304 | tf_op jit(solution)/shard_map/up_rest/pallas_call | solution.py:316
  328.8 40.5 %down.5 = (f32[256,1536]{1,0:T(8,128)}, bf16[256,1536]{1,0:T(8,128)(2,1)}, bf16[256,1536]{1,0:T(8,128)(2,1)}, bf16[256,1536]{1,0:T(8,128)(2,1)}, bf16[256,1536]{1,0:T(8,128)(2,1)}, /*index=5*/bf16[256,1536]{1,0:T(8,128)(2,1)}) custom-call(s32[128]{0:T(128)} %bitcast.19, s32[1]{0:T(128)} %constant.0.clone.1.begin, ...), custom_call_target="tpu_custom_call" | custom-call | flops 42278584320 | bytes 93585408 | tf_op jit(solution)/shard_map/down/pallas_call | solution.py:401
  369.4 51.1 %collective-permute-start.9 = (bf16[256,1536]{1,0:T(8,128)(2,1)}, bf16[256,1536]{1,0:T(8,128)(2,1)}, u32[]{:S(2)}, u32[]{:S(2)}) collective-permute-start(bf16[256,1536]{1,0:T(8,128)(2,1)} %get-tuple-element.64), channel_id=1, source_target_pairs={{0,5},{1,4},{2,7},{3,6},{4,1},{5,0},{6,3},{7,2}} | collective-permute-start | bytes 2359304 | tf_op jit(solution)/shard_map/ppermute | solution.py:428
  420.5 4.9 collective-permute-start.8
  427.3 40.5 %down.6 = (f32[256,1536]{1,0:T(8,128)}, bf16[256,1536]{1,0:T(8,128)(2,1)}, bf16[256,1536]{1,0:T(8,128)(2,1)}, bf16[256,1536]{1,0:T(8,128)(2,1)}, bf16[256,1536]{1,0:T(8,128)(2,1)}, /*index=5*/bf16[256,1536]{1,0:T(8,128)(2,1)}) custom-call(s32[128]{0:T(128)} %bitcast.20, s32[1]{0:T(128)} %constant.1.clone.1.begin, ...), custom_call_target="tpu_custom_call" | custom-call | flops 42278584320 | bytes 93585408 | tf_op jit(solution)/shard_map/down/pallas_call | solution.py:401
  467.8 40.8 %down.7 = (f32[256,1536]{1,0:T(8,128)}, bf16[256,1536]{1,0:T(8,128)(2,1)}, bf16[256,1536]{1,0:T(8,128)(2,1)}, bf16[256,1536]{1,0:T(8,128)(2,1)}, bf16[256,1536]{1,0:T(8,128)(2,1)}, /*index=5*/bf16[256,1536]{1,0:T(8,128)(2,1)}) custom-call(s32[128]{0:T(128)} %bitcast.21, s32[1]{0:T(128)} %constant.2.clone.1.begin, ...), custom_call_target="tpu_custom_call" | custom-call | flops 42278584320 | bytes 93585408 | tf_op jit(solution)/shard_map/down/pallas_call | solution.py:401
  508.6 30.3 %down.8 = (f32[256,1024]{1,0:T(8,128)}, bf16[256,1024]{1,0:T(8,128)(2,1)}, bf16[256,1024]{1,0:T(8,128)(2,1)}, bf16[256,1024]{1,0:T(8,128)(2,1)}, bf16[256,1024]{1,0:T(8,128)(2,1)}, /*index=5*/bf16[256,1024]{1,0:T(8,128)(2,1)}) custom-call(s32[128]{0:T(128)} %bitcast.22, s32[1]{0:T(128)} %constant.3.clone.1.begin, ...), custom_call_target="tpu_custom_call" | custom-call | flops 28185722880 | bytes 71565312 | tf_op jit(solution)/shard_map/down/pallas_call | solution.py:401
  538.9 36.3 %collective-permute-start.14 = (bf16[256,1536]{1,0:T(8,128)(2,1)}, bf16[256,1536]{1,0:T(8,128)(2,1)}, u32[]{:S(2)}, u32[]{:S(2)}) collective-permute-start(bf16[256,1536]{1,0:T(8,128)(2,1)} %get-tuple-element.70), channel_id=1, source_target_pairs={{0,5},{1,4},{2,7},{3,6},{4,1},{5,0},{6,3},{7,2}} | collective-permute-start | bytes 2359304 | tf_op jit(solution)/shard_map/ppermute | solution.py:428
  578.7 19.5 %down.9 = (f32[256,512]{1,0:T(8,128)}, bf16[256,512]{1,0:T(8,128)(2,1)}, bf16[256,512]{1,0:T(8,128)(2,1)}, bf16[256,512]{1,0:T(8,128)(2,1)}, bf16[256,512]{1,0:T(8,128)(2,1)}, /*index=5*/bf16[256,512]{1,0:T(8,128)(2,1)}) custom-call(s32[128]{0:T(128)} %bitcast.23, s32[1]{0:T(128)} %constant.4.clone.1.begin, bf16[768,10752]{1,0:T(8,128)(2,1)} %get-tuple-element.56.one_ref, ...), custom_call_target="tpu_custom_call" | custom-call | flops 14092861440 | bytes 49545216 | tf_op jit(solution)/shard_map/down/pallas_call | solution.py:401
  598.3 5.2 collective-permute-start.19
  603.5 8.9 %collective-permute-done.13 = bf16[256,1536]{1,0:T(8,128)(2,1)} collective-permute-done((bf16[256,1536]{1,0:T(8,128)(2,1)}, bf16[256,1536]{1,0:T(8,128)(2,1)}, u32[]{:S(2)}, u32[]{:S(2)}) %collective-permute-start.13) | collective-permute-done | bytes 786464 | tf_op jit(solution)/shard_map/ppermute | solution.py:428
  614.7 2.8 fusion
  617.6 2.9 fusion.1
  620.5 6.7 collective-permute-done.19
  629.3 16.7 %collective-permute-done.18 = bf16[256,1536]{1,0:T(8,128)(2,1)S(1)} collective-permute-done((bf16[256,1536]{1,0:T(8,128)(2,1)}, bf16[256,1536]{1,0:T(8,128)(2,1)S(1)}, u32[]{:S(2)}, u32[]{:S(2)}) %collective-permute-start.18) | collective-permute-done | bytes 786464 | tf_op jit(solution)/shard_map/ppermute | solution.py:428
  649.5 5.7 collective-permute-done.24
  657.4 11.1 %collective-permute-done.23 = bf16[256,1024]{1,0:T(8,128)(2,1)S(1)} collective-permute-done((bf16[256,1024]{1,0:T(8,128)(2,1)S(1)}, bf16[256,1024]{1,0:T(8,128)(2,1)S(1)}, u32[]{:S(2)}, u32[]{:S(2)}) %collective-permute-start.23) | collective-permute-done | bytes 524320 | tf_op jit(solution)/shard_map/ppermute | solution.py:428
  672.1 5.8 collective-permute-done.28
  677.8 3.1 collective-permute-done.26
  (81 shorter events, 27.2 us)
Async XLA Ops:
  8.5 70.6 %collective-permute-start.1 = (bf16[256,6144]{1,0:T(8,128)(2,1)}, bf16[256,6144]{1,0:T(8,128)(2,1)}, u32[]{:S(2)}, u32[]{:S(2)}) collective-permute-start(bf16[256,6144]{1,0:T(8,128)(2,1)} %bitcast.13), channel_id=1, source_target_pairs={{0,2},{1,3},{2,0},{3,1},{4,6},{5,7},{6,4},{7,5}} | collective-permute-start | bytes 9437192 | tf_op jit(solution)/shard_map/ppermute | solution.py:428
  10.4 70.2 %collective-permute-start.2 = (bf16[256,6144]{1,0:T(8,128)(2,1)}, bf16[256,6144]{1,0:T(8,128)(2,1)}, u32[]{:S(2)}, u32[]{:S(2)}) collective-permute-start(bf16[256,6144]{1,0:T(8,128)(2,1)} %bitcast.14), channel_id=1, source_target_pairs={{0,4},{1,5},{2,6},{3,7},{4,0},{5,1},{6,2},{7,3}} | collective-permute-start | bytes 9437192 | tf_op jit(solution)/shard_map/ppermute | solution.py:428
  80.5 15.6 %collective-permute-start.3 = (bf16[256,6144]{1,0:T(8,128)(2,1)}, bf16[256,6144]{1,0:T(8,128)(2,1)}, u32[]{:S(2)}, u32[]{:S(2)}) collective-permute-start(bf16[256,6144]{1,0:T(8,128)(2,1)} %collective-permute-done.1.refs_2_), channel_id=1, source_target_pairs={{0,1},{1,0},{2,3},{3,2},{4,5},{5,4},{6,7},{7,6}} | collective-permute-start | bytes 9437192 | tf_op jit(solution)/shard_map/ppermute | solution.py:428
  369.4 169.5 %collective-permute-start.9 = (bf16[256,1536]{1,0:T(8,128)(2,1)}, bf16[256,1536]{1,0:T(8,128)(2,1)}, u32[]{:S(2)}, u32[]{:S(2)}) collective-permute-start(bf16[256,1536]{1,0:T(8,128)(2,1)} %get-tuple-element.64), channel_id=1, source_target_pairs={{0,5},{1,4},{2,7},{3,6},{4,1},{5,0},{6,3},{7,2}} | collective-permute-start | bytes 2359304 | tf_op jit(solution)/shard_map/ppermute | solution.py:428
  420.5 154.8 %collective-permute-start.8 = (bf16[256,1536]{1,0:T(8,128)(2,1)}, bf16[256,1536]{1,0:T(8,128)(2,1)}, u32[]{:S(2)}, u32[]{:S(2)}) collective-permute-start(bf16[256,1536]{1,0:T(8,128)(2,1)} %get-tuple-element.63), channel_id=1, source_target_pairs={{0,4},{1,5},{2,6},{3,7},{4,0},{5,1},{6,2},{7,3}} | collective-permute-start | bytes 2359304 | tf_op jit(solution)/shard_map/ppermute | solution.py:428
  425.4 151.4 %collective-permute-start.7 = (bf16[256,1536]{1,0:T(8,128)(2,1)}, bf16[256,1536]{1,0:T(8,128)(2,1)}, u32[]{:S(2)}, u32[]{:S(2)}) collective-permute-start(bf16[256,1536]{1,0:T(8,128)(2,1)} %get-tuple-element.62), channel_id=1, source_target_pairs={{0,3},{1,2},{2,1},{3,0},{4,7},{5,6},{6,5},{7,4}} | collective-permute-start | bytes 2359304 | tf_op jit(solution)/shard_map/ppermute | solution.py:428
  425.4 151.5 %collective-permute-start.6 = (bf16[256,1536]{1,0:T(8,128)(2,1)}, bf16[256,1536]{1,0:T(8,128)(2,1)}, u32[]{:S(2)}, u32[]{:S(2)}) collective-permute-start(bf16[256,1536]{1,0:T(8,128)(2,1)} %get-tuple-element.61), channel_id=1, source_target_pairs={{0,2},{1,3},{2,0},{3,1},{4,6},{5,7},{6,4},{7,5}} | collective-permute-start | bytes 2359304 | tf_op jit(solution)/shard_map/ppermute | solution.py:428
  425.5 151.6 %collective-permute-start.5 = (bf16[256,1536]{1,0:T(8,128)(2,1)}, bf16[256,1536]{1,0:T(8,128)(2,1)}, u32[]{:S(2)}, u32[]{:S(2)}) collective-permute-start(bf16[256,1536]{1,0:T(8,128)(2,1)} %get-tuple-element.60), channel_id=1, source_target_pairs={{0,1},{1,0},{2,3},{3,2},{4,5},{5,4},{6,7},{7,6}} | collective-permute-start | bytes 2359304 | tf_op jit(solution)/shard_map/ppermute | solution.py:428
  538.9 59.3 %collective-permute-start.14 = (bf16[256,1536]{1,0:T(8,128)(2,1)}, bf16[256,1536]{1,0:T(8,128)(2,1)}, u32[]{:S(2)}, u32[]{:S(2)}) collective-permute-start(bf16[256,1536]{1,0:T(8,128)(2,1)} %get-tuple-element.70), channel_id=1, source_target_pairs={{0,5},{1,4},{2,7},{3,6},{4,1},{5,0},{6,3},{7,2}} | collective-permute-start | bytes 2359304 | tf_op jit(solution)/shard_map/ppermute | solution.py:428
  575.3 37.2 %collective-permute-start.13 = (bf16[256,1536]{1,0:T(8,128)(2,1)}, bf16[256,1536]{1,0:T(8,128)(2,1)}, u32[]{:S(2)}, u32[]{:S(2)}) collective-permute-start(bf16[256,1536]{1,0:T(8,128)(2,1)} %get-tuple-element.69), channel_id=1, source_target_pairs={{0,4},{1,5},{2,6},{3,7},{4,0},{5,1},{6,2},{7,3}} | collective-permute-start | bytes 2359304 | tf_op jit(solution)/shard_map/ppermute | solution.py:428
  576.9 36.0 %collective-permute-start.12 = (bf16[256,1536]{1,0:T(8,128)(2,1)}, bf16[256,1536]{1,0:T(8,128)(2,1)}, u32[]{:S(2)}, u32[]{:S(2)}) collective-permute-start(bf16[256,1536]{1,0:T(8,128)(2,1)} %get-tuple-element.68), channel_id=1, source_target_pairs={{0,3},{1,2},{2,1},{3,0},{4,7},{5,6},{6,5},{7,4}} | collective-permute-start | bytes 2359304 | tf_op jit(solution)/shard_map/ppermute | solution.py:428
  576.9 36.0 %collective-permute-start.11 = (bf16[256,1536]{1,0:T(8,128)(2,1)}, bf16[256,1536]{1,0:T(8,128)(2,1)}, u32[]{:S(2)}, u32[]{:S(2)}) collective-permute-start(bf16[256,1536]{1,0:T(8,128)(2,1)} %get-tuple-element.67), channel_id=1, source_target_pairs={{0,2},{1,3},{2,0},{3,1},{4,6},{5,7},{6,4},{7,5}} | collective-permute-start | bytes 2359304 | tf_op jit(solution)/shard_map/ppermute | solution.py:428
  577.1 35.8 %collective-permute-start.10 = (bf16[256,1536]{1,0:T(8,128)(2,1)}, bf16[256,1536]{1,0:T(8,128)(2,1)}, u32[]{:S(2)}, u32[]{:S(2)}) collective-permute-start(bf16[256,1536]{1,0:T(8,128)(2,1)} %get-tuple-element.66), channel_id=1, source_target_pairs={{0,1},{1,0},{2,3},{3,2},{4,5},{5,4},{6,7},{7,6}} | collective-permute-start | bytes 2359304 | tf_op jit(solution)/shard_map/ppermute | solution.py:428
  598.3 28.9 %collective-permute-start.19 = (bf16[256,1536]{1,0:T(8,128)(2,1)}, bf16[256,1536]{1,0:T(8,128)(2,1)S(1)}, u32[]{:S(2)}, u32[]{:S(2)}) collective-permute-start(bf16[256,1536]{1,0:T(8,128)(2,1)} %get-tuple-element.76), channel_id=1, source_target_pairs={{0,5},{1,4},{2,7},{3,6},{4,1},{5,0},{6,3},{7,2}} | collective-permute-start | bytes 2359304 | tf_op jit(solution)/shard_map/ppermute | solution.py:428
  612.4 33.6 %collective-permute-start.18 = (bf16[256,1536]{1,0:T(8,128)(2,1)}, bf16[256,1536]{1,0:T(8,128)(2,1)S(1)}, u32[]{:S(2)}, u32[]{:S(2)}) collective-permute-start(bf16[256,1536]{1,0:T(8,128)(2,1)} %get-tuple-element.75), channel_id=1, source_target_pairs={{0,4},{1,5},{2,6},{3,7},{4,0},{5,1},{6,2},{7,3}} | collective-permute-start | bytes 2359304 | tf_op jit(solution)/shard_map/ppermute | solution.py:428
  612.8 33.6 %collective-permute-start.17 = (bf16[256,1536]{1,0:T(8,128)(2,1)}, bf16[256,1536]{1,0:T(8,128)(2,1)S(1)}, u32[]{:S(2)}, u32[]{:S(2)}) collective-permute-start(bf16[256,1536]{1,0:T(8,128)(2,1)} %get-tuple-element.74), channel_id=1, source_target_pairs={{0,3},{1,2},{2,1},{3,0},{4,7},{5,6},{6,5},{7,4}} | collective-permute-start | bytes 2359304 | tf_op jit(solution)/shard_map/ppermute | solution.py:428
  612.9 34.1 %collective-permute-start.16 = (bf16[256,1536]{1,0:T(8,128)(2,1)}, bf16[256,1536]{1,0:T(8,128)(2,1)S(1)}, u32[]{:S(2)}, u32[]{:S(2)}) collective-permute-start(bf16[256,1536]{1,0:T(8,128)(2,1)} %get-tuple-element.73), channel_id=1, source_target_pairs={{0,2},{1,3},{2,0},{3,1},{4,6},{5,7},{6,4},{7,5}} | collective-permute-start | bytes 2359304 | tf_op jit(solution)/shard_map/ppermute | solution.py:428
  612.9 35.5 %collective-permute-start.15 = (bf16[256,1536]{1,0:T(8,128)(2,1)}, bf16[256,1536]{1,0:T(8,128)(2,1)S(1)}, u32[]{:S(2)}, u32[]{:S(2)}) collective-permute-start(bf16[256,1536]{1,0:T(8,128)(2,1)} %get-tuple-element.72), channel_id=1, source_target_pairs={{0,1},{1,0},{2,3},{3,2},{4,5},{5,4},{6,7},{7,6}} | collective-permute-start | bytes 2359304 | tf_op jit(solution)/shard_map/ppermute | solution.py:428
  627.2 28.0 %collective-permute-start.24 = (bf16[256,1024]{1,0:T(8,128)(2,1)S(1)}, bf16[256,1024]{1,0:T(8,128)(2,1)S(1)}, u32[]{:S(2)}, u32[]{:S(2)}) collective-permute-start(bf16[256,1024]{1,0:T(8,128)(2,1)S(1)} %copy-done.10), channel_id=1, source_target_pairs={{0,5},{1,4},{2,7},{3,6},{4,1},{5,0},{6,3},{7,2}} | collective-permute-start | bytes 1572872 | tf_op jit(solution)/shard_map/ppermute | solution.py:428
  646.0 22.5 %collective-permute-start.23 = (bf16[256,1024]{1,0:T(8,128)(2,1)S(1)}, bf16[256,1024]{1,0:T(8,128)(2,1)S(1)}, u32[]{:S(2)}, u32[]{:S(2)}) collective-permute-start(bf16[256,1024]{1,0:T(8,128)(2,1)S(1)} %copy-done.9), channel_id=1, source_target_pairs={{0,4},{1,5},{2,6},{3,7},{4,0},{5,1},{6,2},{7,3}} | collective-permute-start | bytes 1572872 | tf_op jit(solution)/shard_map/ppermute | solution.py:428
  646.5 22.5 %collective-permute-start.22 = (bf16[256,1024]{1,0:T(8,128)(2,1)S(1)}, bf16[256,1024]{1,0:T(8,128)(2,1)S(1)}, u32[]{:S(2)}, u32[]{:S(2)}) collective-permute-start(bf16[256,1024]{1,0:T(8,128)(2,1)S(1)} %copy-done.8), channel_id=1, source_target_pairs={{0,3},{1,2},{2,1},{3,0},{4,7},{5,6},{6,5},{7,4}} | collective-permute-start | bytes 1572872 | tf_op jit(solution)/shard_map/ppermute | solution.py:428
  646.9 22.8 %collective-permute-start.21 = (bf16[256,1024]{1,0:T(8,128)(2,1)S(1)}, bf16[256,1024]{1,0:T(8,128)(2,1)S(1)}, u32[]{:S(2)}, u32[]{:S(2)}) collective-permute-start(bf16[256,1024]{1,0:T(8,128)(2,1)S(1)} %copy-done.7), channel_id=1, source_target_pairs={{0,2},{1,3},{2,0},{3,1},{4,6},{5,7},{6,4},{7,5}} | collective-permute-start | bytes 1572872 | tf_op jit(solution)/shard_map/ppermute | solution.py:428
  648.4 22.5 %collective-permute-start.20 = (bf16[256,1024]{1,0:T(8,128)(2,1)S(1)}, bf16[256,1024]{1,0:T(8,128)(2,1)S(1)}, u32[]{:S(2)}, u32[]{:S(2)}) collective-permute-start(bf16[256,1024]{1,0:T(8,128)(2,1)S(1)} %copy-done.6), channel_id=1, source_target_pairs={{0,1},{1,0},{2,3},{3,2},{4,5},{5,4},{6,7},{7,6}} | collective-permute-start | bytes 1572872 | tf_op jit(solution)/shard_map/ppermute | solution.py:428
  655.2 16.9 %collective-permute-start.29 = (bf16[256,512]{1,0:T(8,128)(2,1)S(1)}, bf16[256,512]{1,0:T(8,128)(2,1)S(1)}, u32[]{:S(2)}, u32[]{:S(2)}) collective-permute-start(bf16[256,512]{1,0:T(8,128)(2,1)S(1)} %copy-done.15), channel_id=1, source_target_pairs={{0,5},{1,4},{2,7},{3,6},{4,1},{5,0},{6,3},{7,2}} | collective-permute-start | bytes 786440 | tf_op jit(solution)/shard_map/ppermute | solution.py:428
  (22 other events, 383.4 us)

commit v2 on v1

--- a/solution.py
+++ b/solution.py
@@ -11,9 +11,9 @@
 F32, BF16, I32 = jnp.float32, jnp.bfloat16, jnp.int32
 MESH = pl.DeviceIdType.MESH
 VMEM_LIMIT = 62 * 2**20
-CHUNKS = (1536, 1536, 1536, 1024, 512)
+CHUNKS = (2560, 2048, 1536)
 NEAR_BLOCK, REST_BLOCK, DOWN_BLOCK = 512, 512, 256
-NEAR_SIZES = (192, 256, 320)
+NEAR_ROWS = 160
 NEAR_STEPS = 15
 ROW_CHUNKS = (192, 224, 256, 288, 320)
 SOURCES = 6
@@ -154,18 +154,10 @@
         def step(k, _):
             at = pl.ds(pl.multiple_of(k * block, block), block)
             z = jnp.dot(pick, x_ref[:, at], preferred_element_type=F32).astype(BF16)
-            z_ref[pl.ds(low, 16), at] += z[:16]
-            z_ref[pl.ds(pl.multiple_of(low + 16, 16), window - 16), at] = z[16:]
+            z_ref[pl.ds(low, window), at] += z
             return 0
 
         lax.fori_loop(0, d // block, step, 0)
-
-
-def sizes_do(sizes, n, body):
-    for k, size in enumerate(sizes):
-        low = n > sizes[k - 1] if k else n >= 0
-        high = n <= size if k + 1 < len(sizes) else n >= 0
-        pl.when(low & high)(functools.partial(body, size))
 
 
 def chunks_do(rows, body):
@@ -203,17 +195,23 @@
         for s, ref in enumerate((x_ref, mate_ref)):
             place_rows(window, ref, pos_ref[s : s + 1, :], num[START + s], num[COUNT + s], z)
 
-    def body(m):
-        h_ref[0:m] = swiglu(z[0:m], wg_ref[...], wu_ref[...])
-        if m < h_ref.shape[0]:
-            h_ref[m:] = jnp.zeros((h_ref.shape[0] - m, h_ref.shape[1]), BF16)
-
-    sizes_do(NEAR_SIZES, num[NEAR], body)
+    two = num[NEAR] > NEAR_ROWS
+
+    @pl.when(jnp.logical_not(two))
+    def _():
+        h_ref[NEAR_ROWS:] = jnp.zeros((NEAR_ROWS, h_ref.shape[1]), BF16)
+
+    def chunk(t, _):
+        at = pl.ds(pl.multiple_of(t * NEAR_ROWS, 32), NEAR_ROWS)
+        h_ref[at] = swiglu(z[at], wg_ref[...], wu_ref[...])
+        return 0
+
+    lax.fori_loop(0, jnp.where(two, 2, 1), chunk, 0)
 
 
 def up_near(num, x, mate, pos, scale, wg, wu, slots):
     tokens, d = x.shape
-    window, rows = slots + 16, NEAR_SIZES[-1]
+    window, rows = slots + 16, 2 * NEAR_ROWS
     whole = pl.BlockSpec((tokens, d), lambda j, num: (0, 0), pipeline_mode=pl.Buffered(1))
     weights = pl.BlockSpec((None, d, NEAR_BLOCK), lambda j, num: (num[FIRST], 0, j))
     return pl.pallas_call(
@@ -250,23 +248,26 @@
     j = pl.program_id(0)
     copies = [pltpu.make_async_copy(sources[s], xs[s], sems.at[s]) for s in range(SOURCES)]
 
-    def fill(e, fresh):
+    order = (2, 4, 3, 5, 0, 1)
+
+    @pl.when(j == 0)
+    def _():
+        for s in order[:2]:
+            copies[s].start()
+
+    @pl.when((j == 0) | (j == steps))
+    def _():
         z[...] = jnp.zeros_like(z)
-        for s in range(SOURCES):
-            if fresh:
+        for k, s in enumerate(order):
+
+            @pl.when(j == 0)
+            def _():
                 copies[s].wait()
-            row = 8 * e + s
-            place_rows(window, xs[s], pos_ref[row : row + 1, :], num[START + row], num[COUNT + row], z)
-
-    @pl.when(j == 0)
-    def _():
-        for copy in copies:
-            copy.start()
-        fill(0, True)
-
-    @pl.when(j == steps)
-    def _():
-        fill(1, False)
+                if k + 2 < SOURCES:
+                    copies[order[k + 2]].start()
+
+            row = jnp.where(j == 0, s, 8 + s)
+            place_rows(window, xs[s], pos_ref[pl.ds(row, 1), :], num[START + row], num[COUNT + row], z)
 
     near_rows = near_ref.shape[0]
     first = j < steps

time: 690 us -> 646 us (0.936)
  Pallas kernels: 474 us -> 445 us
    pallas_call x5 -> x3, Pallas kernels: 172 us -> 153 us  [down(): pl.pallas_call(down_kernel, out_shape=[jax.ShapeDtypeStruct((tokens, size...]
    pallas_call x1, Pallas kernels: 228 us -> 221 us  [up_rest(): pl.pallas_call(functools.partial(up_rest_kernel, window, steps), out_shap...]
    convert_element_type x0 -> x3, other arithmetic: none -> 7.48 us  [layer(): parts.append(y.astype(BF16))]
    ppermute x30 -> x20, waiting for transfers between devices: 72.1 us -> 65.4 us  [swap(): return lax.ppermute(v, ('dp', 'ep'), pairs)]
    ppermute x30 -> x20, starting transfers between devices: 128 us -> 122 us  [swap(): return lax.ppermute(v, ('dp', 'ep'), pairs)]
  transfers between devices with their start and end apart: 30 -> 20, of which waited for: 14 -> 7; matrix products, arithmetic and copies ran while one was open for 1% -> 1% of each run, Pallas kernels for 30% -> 29%
where the time goes in v2:
time: 646 us; the launch traced here: 642 us
  Pallas kernels  445 us (69%)
  starting transfers between devices  122 us (19%)
  waiting for transfers between devices  65.4 us (10%)
  other arithmetic  9.32 us (1%)
    pallas_call x1, Pallas kernels, up_rest(): pl.pallas_call(functools.partial(up_rest_kernel, window, steps), out_shap...  221 us
    pallas_call x3, Pallas kernels, down(): pl.pallas_call(down_kernel, out_shape=[jax.ShapeDtypeStruct((tokens, size...  153 us
    ppermute x20, starting transfers between devices, swap(): return lax.ppermute(v, ('dp', 'ep'), pairs)  122 us
    ppermute x20, waiting for transfers between devices, swap(): return lax.ppermute(v, ('dp', 'ep'), pairs)  65.4 us
    pallas_call x1, Pallas kernels, up_near(): pl.pallas_call(functools.partial(up_near_kernel, window), out_shape=[jax....  64.3 us
  transfers between devices with their start and end apart: 20, of which 7 were waited for; matrix products, arithmetic and copies ran while one was open for 1% of the time, Pallas kernels for 29%

profile of v2, /device:TPU:0, one launch (start us, length us, event | category | flops | bytes accessed | tf_op | source)
XLA Modules:
  0.0 642.5 jit_solution(6533813683119838907)
XLA Ops:
  0.8 7.7 %plan.1 = (s32[16,256]{1,0:T(8,128)}, f32[16,256]{1,0:T(8,128)}, s32[1,128]{1,0:T(1,128)}) custom-call(s32[4,256]{1,0:T(4,128)} %bitcast.23, s32[4,256]{1,0:T(4,128)} %bitcast.24, f32[4,256]{1,0:T(4,128)} %bitcast.25), custom_call_target="tpu_custom_call" | custom-call | flops 10000000 | bytes 100000 | tf_op jit(solution)/shard_map/plan/pallas_call | solution.py:122
  8.5 1.9 collective-permute-start.2
  10.4 1.5 collective-permute-start.1
  11.9 64.3 %up_near.1 = (bf16[320,7680]{1,0:T(8,128)(2,1)}, bf16[12,256,176]{2,1,0:T(8,128)(2,1)}) custom-call(s32[128]{0:T(128)} %bitcast.18, bf16[256,6144]{1,0:T(8,128)(2,1)} %bitcast.16, bf16[256,6144]{1,0:T(8,128)(2,1)} %collective-permute-done.mate_ref.refs_1_, s32[16,256]{1,0:T(8,128)} %get-tuple-element.38.pos_ref.refs_6_, ...), custom_call_target="tpu_custom_call" | custom-call | flops 60397977600 | bytes 188743680 | tf_op jit(solution)/shard_map/up_near/pallas_call | solution.py:217
  76.1 3.0 collective-permute-done.2.refs_4_
  80.6 11.3 %collective-permute-start.3 = (bf16[256,6144]{1,0:T(8,128)(2,1)}, bf16[256,6144]{1,0:T(8,128)(2,1)}, u32[]{:S(2)}, u32[]{:S(2)}) collective-permute-start(bf16[256,6144]{1,0:T(8,128)(2,1)} %collective-permute-done.1.refs_2_), channel_id=1, source_target_pairs={{0,1},{1,0},{2,3},{3,2},{4,5},{5,4},{6,7},{7,6}} | collective-permute-start | bytes 9437192 | tf_op jit(solution)/shard_map/ppermute | solution.py:429
  91.9 5.6 collective-permute-done.3.refs_3_
  97.5 4.5 collective-permute-done.4.refs_5_
  102.0 220.6 %up_rest.1 = (bf16[768,10752]{1,0:T(8,128)(2,1)}, bf16[640,10752]{1,0:T(8,128)(2,1)}) custom-call(s32[128]{0:T(128)} %bitcast.19, bf16[256,6144]{1,0:T(8,128)(2,1)} %bitcast.17, bf16[256,6144]{1,0:T(8,128)(2,1)} %collective-permute-done.mate_ref.refs_1_, bf16[256,6144]{1,0:T(8,128)(2,1)} %collective-permute-done.1.refs_2_, ...), custom_call_target="tpu_custom_call" | custom-call | flops 253671505920 | bytes 528482304 | tf_op jit(solution)/shard_map/up_rest/pallas_call | solution.py:317
  322.6 40.5 %down.5 = (f32[256,1536]{1,0:T(8,128)}, bf16[256,1536]{1,0:T(8,128)(2,1)}, bf16[256,1536]{1,0:T(8,128)(2,1)}, bf16[256,1536]{1,0:T(8,128)(2,1)}, bf16[256,1536]{1,0:T(8,128)(2,1)}, /*index=5*/bf16[256,1536]{1,0:T(8,128)(2,1)}) custom-call(s32[128]{0:T(128)} %bitcast.20, s32[1]{0:T(128)} %constant.2.clone.1.begin, ...), custom_call_target="tpu_custom_call" | custom-call | flops 42278584320 | bytes 93585408 | tf_op jit(solution)/shard_map/down/pallas_call | solution.py:402
  363.0 55.5 %collective-permute-start.15 = (bf16[256,1536]{1,0:T(8,128)(2,1)}, bf16[256,1536]{1,0:T(8,128)(2,1)S(1)}, u32[]{:S(2)}, u32[]{:S(2)}) collective-permute-start(bf16[256,1536]{1,0:T(8,128)(2,1)} %get-tuple-element.60), channel_id=1, source_target_pairs={{0,1},{1,0},{2,3},{3,2},{4,5},{5,4},{6,7},{7,6}} | collective-permute-start | bytes 2359304 | tf_op jit(solution)/shard_map/ppermute | solution.py:429
  420.0 2.1 collective-permute-start.19
  422.1 50.9 %down.4 = (f32[256,2048]{1,0:T(8,128)}, bf16[256,2048]{1,0:T(8,128)(2,1)}, bf16[256,2048]{1,0:T(8,128)(2,1)}, bf16[256,2048]{1,0:T(8,128)(2,1)}, bf16[256,2048]{1,0:T(8,128)(2,1)}, /*index=5*/bf16[256,2048]{1,0:T(8,128)(2,1)}) custom-call(s32[128]{0:T(128)} %bitcast.21, s32[1]{0:T(128)} %constant.1.clone.1.begin, ...), custom_call_target="tpu_custom_call" | custom-call | flops 56371445760 | bytes 115605504 | tf_op jit(solution)/shard_map/down/pallas_call | solution.py:402
  473.0 18.0 %collective-permute-start.10 = (bf16[256,2048]{1,0:T(8,128)(2,1)}, bf16[256,2048]{1,0:T(8,128)(2,1)}, u32[]{:S(2)}, u32[]{:S(2)}) collective-permute-start(bf16[256,2048]{1,0:T(8,128)(2,1)} %get-tuple-element.54), channel_id=1, source_target_pairs={{0,1},{1,0},{2,3},{3,2},{4,5},{5,4},{6,7},{7,6}} | collective-permute-start | bytes 3145736 | tf_op jit(solution)/shard_map/ppermute | solution.py:429
  492.8 1.7 collective-permute-start.14
  494.5 61.6 %down.3 = (f32[256,2560]{1,0:T(8,128)}, bf16[256,2560]{1,0:T(8,128)(2,1)}, bf16[256,2560]{1,0:T(8,128)(2,1)}, bf16[256,2560]{1,0:T(8,128)(2,1)}, bf16[256,2560]{1,0:T(8,128)(2,1)}, /*index=5*/bf16[256,2560]{1,0:T(8,128)(2,1)}) custom-call(s32[128]{0:T(128)} %bitcast.22, s32[1]{0:T(128)} %constant.0.clone.1.begin, ...), custom_call_target="tpu_custom_call" | custom-call | flops 70464307200 | bytes 137625600 | tf_op jit(solution)/shard_map/down/pallas_call | solution.py:402
  556.1 22.4 %collective-permute-start.5 = (bf16[256,2560]{1,0:T(8,128)(2,1)}, bf16[256,2560]{1,0:T(8,128)(2,1)S(1)}, u32[]{:S(2)}, u32[]{:S(2)}) collective-permute-start(bf16[256,2560]{1,0:T(8,128)(2,1)} %get-tuple-element.48), channel_id=1, source_target_pairs={{0,1},{1,0},{2,3},{3,2},{4,5},{5,4},{6,7},{7,6}} | collective-permute-start | bytes 3932168 | tf_op jit(solution)/shard_map/ppermute | solution.py:429
  580.4 1.6 collective-permute-start.9
  582.0 2.8 add_convert_fusion.2
  584.9 3.7 add_convert_fusion.1
  588.5 21.8 %collective-permute-done.6 = bf16[256,2560]{1,0:T(8,128)(2,1)S(1)} collective-permute-done((bf16[256,2560]{1,0:T(8,128)(2,1)}, bf16[256,2560]{1,0:T(8,128)(2,1)S(1)}, u32[]{:S(2)}, u32[]{:S(2)}) %collective-permute-start.6) | collective-permute-done | bytes 1310752 | tf_op jit(solution)/shard_map/ppermute | solution.py:429
  610.4 26.2 %collective-permute-done.7 = bf16[256,2560]{1,0:T(8,128)(2,1)S(1)} collective-permute-done((bf16[256,2560]{1,0:T(8,128)(2,1)}, bf16[256,2560]{1,0:T(8,128)(2,1)S(1)}, u32[]{:S(2)}, u32[]{:S(2)}) %collective-permute-start.7) | collective-permute-done | bytes 1310752 | tf_op jit(solution)/shard_map/ppermute | solution.py:429
  636.6 2.8 collective-permute-done.9
  640.4 1.8 maximum_bitcast_fusion
  (36 shorter events, 8.4 us)
Async XLA Ops:
  0.0 11.9 %collective-permute-start = (bf16[256,6144]{1,0:T(8,128)(2,1)}, bf16[256,6144]{1,0:T(8,128)(2,1)}, u32[]{:S(2)}, u32[]{:S(2)}) collective-permute-start(bf16[256,6144]{1,0:T(8,128)(2,1)} %bitcast.13), channel_id=1, source_target_pairs={{0,1},{1,0},{2,3},{3,2},{4,5},{5,4},{6,7},{7,6}} | collective-permute-start | bytes 9437192 | tf_op jit(solution)/shard_map/ppermute | solution.py:429
  8.5 70.6 %collective-permute-start.2 = (bf16[256,6144]{1,0:T(8,128)(2,1)}, bf16[256,6144]{1,0:T(8,128)(2,1)}, u32[]{:S(2)}, u32[]{:S(2)}) collective-permute-start(bf16[256,6144]{1,0:T(8,128)(2,1)} %bitcast.14), channel_id=1, source_target_pairs={{0,4},{1,5},{2,6},{3,7},{4,0},{5,1},{6,2},{7,3}} | collective-permute-start | bytes 9437192 | tf_op jit(solution)/shard_map/ppermute | solution.py:429
  10.4 70.2 %collective-permute-start.1 = (bf16[256,6144]{1,0:T(8,128)(2,1)}, bf16[256,6144]{1,0:T(8,128)(2,1)}, u32[]{:S(2)}, u32[]{:S(2)}) collective-permute-start(bf16[256,6144]{1,0:T(8,128)(2,1)} %bitcast.15), channel_id=1, source_target_pairs={{0,2},{1,3},{2,0},{3,1},{4,6},{5,7},{6,4},{7,5}} | collective-permute-start | bytes 9437192 | tf_op jit(solution)/shard_map/ppermute | solution.py:429
  80.6 16.9 %collective-permute-start.3 = (bf16[256,6144]{1,0:T(8,128)(2,1)}, bf16[256,6144]{1,0:T(8,128)(2,1)}, u32[]{:S(2)}, u32[]{:S(2)}) collective-permute-start(bf16[256,6144]{1,0:T(8,128)(2,1)} %collective-permute-done.1.refs_2_), channel_id=1, source_target_pairs={{0,1},{1,0},{2,3},{3,2},{4,5},{5,4},{6,7},{7,6}} | collective-permute-start | bytes 9437192 | tf_op jit(solution)/shard_map/ppermute | solution.py:429
  91.9 10.1 %collective-permute-start.4 = (bf16[256,6144]{1,0:T(8,128)(2,1)}, bf16[256,6144]{1,0:T(8,128)(2,1)}, u32[]{:S(2)}, u32[]{:S(2)}) collective-permute-start(bf16[256,6144]{1,0:T(8,128)(2,1)} %collective-permute-done.2.refs_4_), channel_id=1, source_target_pairs={{0,1},{1,0},{2,3},{3,2},{4,5},{5,4},{6,7},{7,6}} | collective-permute-start | bytes 9437192 | tf_op jit(solution)/shard_map/ppermute | solution.py:429
  363.0 110.0 %collective-permute-start.15 = (bf16[256,1536]{1,0:T(8,128)(2,1)}, bf16[256,1536]{1,0:T(8,128)(2,1)S(1)}, u32[]{:S(2)}, u32[]{:S(2)}) collective-permute-start(bf16[256,1536]{1,0:T(8,128)(2,1)} %get-tuple-element.60), channel_id=1, source_target_pairs={{0,1},{1,0},{2,3},{3,2},{4,5},{5,4},{6,7},{7,6}} | collective-permute-start | bytes 2359304 | tf_op jit(solution)/shard_map/ppermute | solution.py:429
  418.6 72.4 %collective-permute-start.16 = (bf16[256,1536]{1,0:T(8,128)(2,1)}, bf16[256,1536]{1,0:T(8,128)(2,1)S(1)}, u32[]{:S(2)}, u32[]{:S(2)}) collective-permute-start(bf16[256,1536]{1,0:T(8,128)(2,1)} %get-tuple-element.61), channel_id=1, source_target_pairs={{0,2},{1,3},{2,0},{3,1},{4,6},{5,7},{6,4},{7,5}} | collective-permute-start | bytes 2359304 | tf_op jit(solution)/shard_map/ppermute | solution.py:429
  418.6 72.4 %collective-permute-start.17 = (bf16[256,1536]{1,0:T(8,128)(2,1)}, bf16[256,1536]{1,0:T(8,128)(2,1)}, u32[]{:S(2)}, u32[]{:S(2)}) collective-permute-start(bf16[256,1536]{1,0:T(8,128)(2,1)} %get-tuple-element.62), channel_id=1, source_target_pairs={{0,3},{1,2},{2,1},{3,0},{4,7},{5,6},{6,5},{7,4}} | collective-permute-start | bytes 2359304 | tf_op jit(solution)/shard_map/ppermute | solution.py:429
  420.0 72.4 %collective-permute-start.18 = (bf16[256,1536]{1,0:T(8,128)(2,1)}, bf16[256,1536]{1,0:T(8,128)(2,1)}, u32[]{:S(2)}, u32[]{:S(2)}) collective-permute-start(bf16[256,1536]{1,0:T(8,128)(2,1)} %get-tuple-element.63), channel_id=1, source_target_pairs={{0,4},{1,5},{2,6},{3,7},{4,0},{5,1},{6,2},{7,3}} | collective-permute-start | bytes 2359304 | tf_op jit(solution)/shard_map/ppermute | solution.py:429
  420.0 72.8 %collective-permute-start.19 = (bf16[256,1536]{1,0:T(8,128)(2,1)}, bf16[256,1536]{1,0:T(8,128)(2,1)}, u32[]{:S(2)}, u32[]{:S(2)}) collective-permute-start(bf16[256,1536]{1,0:T(8,128)(2,1)} %get-tuple-element.64), channel_id=1, source_target_pairs={{0,5},{1,4},{2,7},{3,6},{4,1},{5,0},{6,3},{7,2}} | collective-permute-start | bytes 2359304 | tf_op jit(solution)/shard_map/ppermute | solution.py:429
  473.0 19.8 %copy-start.3 = (bf16[256,1536]{1,0:T(8,128)(2,1)}, bf16[256,1536]{1,0:T(8,128)(2,1)S(1)}, u32[]{:S(2)}) copy-start(bf16[256,1536]{1,0:T(8,128)(2,1)S(1)} %collective-permute-done.15) | copy-start | bytes 2359300
  473.0 83.1 %collective-permute-start.10 = (bf16[256,2048]{1,0:T(8,128)(2,1)}, bf16[256,2048]{1,0:T(8,128)(2,1)}, u32[]{:S(2)}, u32[]{:S(2)}) collective-permute-start(bf16[256,2048]{1,0:T(8,128)(2,1)} %get-tuple-element.54), channel_id=1, source_target_pairs={{0,1},{1,0},{2,3},{3,2},{4,5},{5,4},{6,7},{7,6}} | collective-permute-start | bytes 3145736 | tf_op jit(solution)/shard_map/ppermute | solution.py:429
  491.0 87.5 %collective-permute-start.11 = (bf16[256,2048]{1,0:T(8,128)(2,1)}, bf16[256,2048]{1,0:T(8,128)(2,1)}, u32[]{:S(2)}, u32[]{:S(2)}) collective-permute-start(bf16[256,2048]{1,0:T(8,128)(2,1)} %get-tuple-element.55), channel_id=1, source_target_pairs={{0,2},{1,3},{2,0},{3,1},{4,6},{5,7},{6,4},{7,5}} | collective-permute-start | bytes 3145736 | tf_op jit(solution)/shard_map/ppermute | solution.py:429
  491.0 87.5 %collective-permute-start.12 = (bf16[256,2048]{1,0:T(8,128)(2,1)}, bf16[256,2048]{1,0:T(8,128)(2,1)}, u32[]{:S(2)}, u32[]{:S(2)}) collective-permute-start(bf16[256,2048]{1,0:T(8,128)(2,1)} %get-tuple-element.56), channel_id=1, source_target_pairs={{0,3},{1,2},{2,1},{3,0},{4,7},{5,6},{6,5},{7,4}} | collective-permute-start | bytes 3145736 | tf_op jit(solution)/shard_map/ppermute | solution.py:429
  492.4 87.5 %collective-permute-start.13 = (bf16[256,2048]{1,0:T(8,128)(2,1)}, bf16[256,2048]{1,0:T(8,128)(2,1)}, u32[]{:S(2)}, u32[]{:S(2)}) collective-permute-start(bf16[256,2048]{1,0:T(8,128)(2,1)} %get-tuple-element.57), channel_id=1, source_target_pairs={{0,4},{1,5},{2,6},{3,7},{4,0},{5,1},{6,2},{7,3}} | collective-permute-start | bytes 3145736 | tf_op jit(solution)/shard_map/ppermute | solution.py:429
  492.8 89.2 %copy-start.2 = (f32[256,1536]{1,0:T(8,128)S(1)}, f32[256,1536]{1,0:T(8,128)}, u32[]{:S(2)}) copy-start(f32[256,1536]{1,0:T(8,128)} %get-tuple-element.59) | copy-start | bytes 4718596
  492.8 87.6 %collective-permute-start.14 = (bf16[256,2048]{1,0:T(8,128)(2,1)}, bf16[256,2048]{1,0:T(8,128)(2,1)}, u32[]{:S(2)}, u32[]{:S(2)}) collective-permute-start(bf16[256,2048]{1,0:T(8,128)(2,1)} %get-tuple-element.58), channel_id=1, source_target_pairs={{0,5},{1,4},{2,7},{3,6},{4,1},{5,0},{6,3},{7,2}} | collective-permute-start | bytes 3145736 | tf_op jit(solution)/shard_map/ppermute | solution.py:429
  556.1 32.4 %collective-permute-start.5 = (bf16[256,2560]{1,0:T(8,128)(2,1)}, bf16[256,2560]{1,0:T(8,128)(2,1)S(1)}, u32[]{:S(2)}, u32[]{:S(2)}) collective-permute-start(bf16[256,2560]{1,0:T(8,128)(2,1)} %get-tuple-element.48), channel_id=1, source_target_pairs={{0,1},{1,0},{2,3},{3,2},{4,5},{5,4},{6,7},{7,6}} | collective-permute-start | bytes 3932168 | tf_op jit(solution)/shard_map/ppermute | solution.py:429
  578.5 31.9 %collective-permute-start.6 = (bf16[256,2560]{1,0:T(8,128)(2,1)}, bf16[256,2560]{1,0:T(8,128)(2,1)S(1)}, u32[]{:S(2)}, u32[]{:S(2)}) collective-permute-start(bf16[256,2560]{1,0:T(8,128)(2,1)} %get-tuple-element.49), channel_id=1, source_target_pairs={{0,2},{1,3},{2,0},{3,1},{4,6},{5,7},{6,4},{7,5}} | collective-permute-start | bytes 3932168 | tf_op jit(solution)/shard_map/ppermute | solution.py:429
  578.5 58.1 %collective-permute-start.7 = (bf16[256,2560]{1,0:T(8,128)(2,1)}, bf16[256,2560]{1,0:T(8,128)(2,1)S(1)}, u32[]{:S(2)}, u32[]{:S(2)}) collective-permute-start(bf16[256,2560]{1,0:T(8,128)(2,1)} %get-tuple-element.50), channel_id=1, source_target_pairs={{0,3},{1,2},{2,1},{3,0},{4,7},{5,6},{6,5},{7,4}} | collective-permute-start | bytes 3932168 | tf_op jit(solution)/shard_map/ppermute | solution.py:429
  579.9 56.7 %collective-permute-start.8 = (bf16[256,2560]{1,0:T(8,128)(2,1)}, bf16[256,2560]{1,0:T(8,128)(2,1)S(1)}, u32[]{:S(2)}, u32[]{:S(2)}) collective-permute-start(bf16[256,2560]{1,0:T(8,128)(2,1)} %get-tuple-element.51), channel_id=1, source_target_pairs={{0,4},{1,5},{2,6},{3,7},{4,0},{5,1},{6,2},{7,3}} | collective-permute-start | bytes 3932168 | tf_op jit(solution)/shard_map/ppermute | solution.py:429
  580.4 59.0 %collective-permute-start.9 = (bf16[256,2560]{1,0:T(8,128)(2,1)}, bf16[256,2560]{1,0:T(8,128)(2,1)S(1)}, u32[]{:S(2)}, u32[]{:S(2)}) collective-permute-start(bf16[256,2560]{1,0:T(8,128)(2,1)} %get-tuple-element.52), channel_id=1, source_target_pairs={{0,5},{1,4},{2,7},{3,6},{4,1},{5,0},{6,3},{7,2}} | collective-permute-start | bytes 3932168 | tf_op jit(solution)/shard_map/ppermute | solution.py:429
  582.0 2.8 copy-start.1
  584.8 54.6 %copy-start = (f32[256,2560]{1,0:T(8,128)S(1)}, f32[256,2560]{1,0:T(8,128)}, u32[]{:S(2)}) copy-start(f32[256,2560]{1,0:T(8,128)} %get-tuple-element.47) | copy-start | bytes 7864324
  (1 other events, 1.8 us)
